TPU v7x, 32 devices: a whole 2x2x4 slice. The times are simulated.
32 devices in a mesh: groups: 2 (over y), az: 4 (over z), rg: 2 (over x), acq: 2 (over core).
Axes of the slice: x: 2, y: 2, z: 4, core: 2. Of those that a mesh axis runs over, the one named last changes fastest.
Arguments:
- image_stack: bfloat16 [2, 64, 32, 4, 256], P(None, ('az', 'acq'), 'groups', 'rg'), parts along dimension 2, may hold values from -12 to 12
- steering: bfloat16 [4, 2, 64, 512], P('rg'), as said below
- wiener_filter: bfloat16 [4, 2, 64, 64], P('rg'), may hold values from -0.5 to 0.5
- range_group: int32 [4], P('rg'), may hold values from 0 to 3, as said below
- lay_list: int32 [32, 4, 32], P(('groups', 'az', 'acq'), 'rg'), parts along dimension 0, may hold values from 0 to 255, as said below
- lay_count: int32 [32, 4], P(('groups', 'az', 'acq'), 'rg'), parts along dimension 0, may hold values from 0 to 32, as said below
Outputs:
- power: bfloat16 [32, 4, 512, 256], P(('groups', 'az', 'acq'), 'rg'), parts along dimension 0
There are 2 independent parts, one for each index of `groups`. A program takes and returns all parts, laid end to end along the dimension named above; an argument that names none is the same for every part. Nothing has to cross between parts.
Inputs may be any that keep to these rules, and one draw needn't show every extreme that they name: `lay_list`: within one block the 32 entries are distinct pixels. The first lay_count entries of a block's list are its layover pixels; some block has 32. `range_group`: range block r belongs to a group from (r // 2) * 2 to (r // 2) * 2 + 1. `steering`: every complex entry has modulus 1 / sqrt(512) up to rounding.
All inputs are finite; a program needn't handle non-finite values.
Results may differ from a plain program's by a relative error of at most 0.0075.
Values may be sent and summed in bfloat16 or wider, within the bound.
A program may use at most 64 MiB of HBM per device.

v0:
```python
import functools

import jax
import jax.numpy as jnp
from jax import lax
from jax.experimental import pallas as pl
from jax.experimental.pallas import tpu as pltpu
from jax.sharding import PartitionSpec as P

ITERS = 8
STEP_SIZE = 0.5
SHRINK = 0.25
LANES = 128
VMEM_LIMIT = 16 * 1024 * 1024
MESH = pl.DeviceIdType.MESH


def iota(shape, axis):
    return lax.broadcasted_iota(jnp.int32, shape, axis)


def exchange_kernel(
    n_az,
    n_acq,
    range_group_in,
    lay_count_in,
    image,
    steering_in,
    wiener_filter_in,
    lay_list_in,
    recv,
    op,
    op_t,
    mix,
    chosen,
    lane_mask,
    covered,
    gather,
    range_group,
    lay_count,
    steering,
    wiener_filter,
    lay_list,
    send_sem,
    recv_sem,
    local_sem,
):
    n = n_az * n_acq
    me = lax.axis_index("az") * n_acq + lax.axis_index("acq")
    halves, share, azb_all, ranges, pixels = image.shape
    blocks = azb_all // n
    groups, _, acqs, elevation = steering.shape
    rows = halves * acqs
    wide = ranges * rows
    listed = lay_list.shape[2]
    lanes = blocks * ranges * listed
    sets = blocks * ranges
    spread = rows * sets
    chunks = elevation // LANES
    bf16 = jnp.bfloat16
    f32 = jnp.float32

    def peer(index):
        return {"az": index // n_acq, "acq": lax.rem(index, n_acq)}

    barrier = pltpu.get_barrier_semaphore()
    for offset in range(1, n):
        pl.semaphore_signal(
            barrier, inc=1, device_id=peer(lax.rem(me + offset, n)), device_id_type=MESH
        )
    inputs = []
    for at, (source, target) in enumerate(
        (
            (range_group_in, range_group),
            (lay_count_in, lay_count),
            (steering_in, steering),
            (wiener_filter_in, wiener_filter),
            (lay_list_in, lay_list),
        )
    ):
        copy = pltpu.make_async_copy(source, target, local_sem.at[at + 1])
        copy.start()
        inputs.append(copy)
    local = pltpu.make_async_copy(
        image.at[:, :, pl.ds(blocks * me, blocks)],
        recv.at[:, pl.ds(share * me, share)],
        local_sem.at[0],
    )
    local.start()

    first_group = lax.axis_index("rg") * groups
    copy_rows = (iota((rows, spread), 1) // sets == iota((rows, spread), 0)).astype(bf16)
    at_row, at_column = iota((spread, wide), 0), iota((spread, wide), 1)
    gather[...] = (
        (at_row // sets == lax.rem(at_column, rows))
        & (lax.rem(at_row, ranges) == at_column // rows)
    ).astype(bf16)
    lane_range = lax.rem(iota((lanes, wide), 0) // listed, ranges)
    lane_mask[...] = jnp.where(lane_range == iota((lanes, wide), 1) // rows, STEP_SIZE, 0.0)
    for copy in inputs:
        copy.wait()
    for r in range(ranges):
        group = range_group[r] - first_group
        steer = steering[0]
        filt = wiener_filter[0]
        for g in range(1, groups):
            steer = jnp.where(group == g, steering[g], steer)
            filt = jnp.where(group == g, wiener_filter[g], filt)
        re, im = steer[0], steer[1]
        top = r * rows
        for j in range(chunks):
            cut = slice(j * LANES, (j + 1) * LANES)
            left = slice(2 * j * LANES, (2 * j + 1) * LANES)
            right = slice((2 * j + 1) * LANES, (2 * j + 2) * LANES)
            op[top : top + acqs, left] = re[:, cut]
            op[top : top + acqs, right] = -im[:, cut]
            op[top + acqs : top + rows, left] = im[:, cut]
            op[top + acqs : top + rows, right] = re[:, cut]
        upper = jnp.concatenate([filt[0], -filt[1]], axis=1)
        lower = jnp.concatenate([filt[1], filt[0]], axis=1)
        filter_matrix = jnp.concatenate([upper, lower], axis=0)
        repeated = jnp.dot(filter_matrix, copy_rows, preferred_element_type=f32)
        for b in range(blocks):
            keep = lax.rem(iota((rows, spread), 1), sets) == b * ranges + r
            at = (b * ranges + r) * rows
            mix[at : at + rows, :] = jnp.where(keep, repeated, 0.0).astype(bf16)
    for j in range(2 * chunks):
        op_t[j * LANES : (j + 1) * LANES, :] = op[:, j * LANES : (j + 1) * LANES].T

    diagonal = iota((listed, listed), 0) == iota((listed, listed), 1)
    for b in range(blocks):
        for r in range(ranges):
            entries = lay_list[b, r : r + 1, :].astype(f32)
            column = jnp.sum(jnp.where(diagonal, entries, 0.0), axis=1, keepdims=True)
            alive = iota((listed, pixels), 0) < lay_count[b, r]
            hit = (iota((listed, pixels), 1).astype(f32) == column) & alive
            hot = jnp.where(hit, 1.0, 0.0)
            at = b * ranges + r
            chosen[at * listed : (at + 1) * listed, :] = hot.astype(bf16)
            covered[at : at + 1, :] = jnp.sum(hot, axis=0, keepdims=True)

    pl.semaphore_wait(barrier, n - 1)
    copies = []
    for offset in range(1, n):
        there = lax.rem(me + offset, n)
        copy = pltpu.make_async_remote_copy(
            src_ref=image.at[:, :, pl.ds(blocks * there, blocks)],
            dst_ref=recv.at[:, pl.ds(share * me, share)],
            send_sem=send_sem.at[offset],
            recv_sem=recv_sem.at[offset],
            device_id=peer(there),
            device_id_type=MESH,
        )
        copy.start()
        copies.append(copy)
    local.wait()
    for copy in copies:
        copy.wait()


def solve_kernel(
    ranges,
    recv,
    op,
    op_t,
    mix,
    chosen,
    lane_mask,
    covered,
    gather,
    power,
    estimate,
    rounded,
    beams,
    result,
    out_sem,
):
    spread = mix.shape[0]
    wide = op.shape[0]
    rows = wide // ranges
    sets = spread // rows
    chunks = op.shape[1] // (2 * LANES)
    lanes, pixels = chosen.shape
    listed = lanes // sets
    bf16 = jnp.bfloat16
    f32 = jnp.float32

    data = recv[...].reshape(spread, pixels)
    picked = lax.dot_general(
        chosen[...], data, (((1,), (1,)), ((), ())), preferred_element_type=f32
    )
    own = iota((lanes, spread), 0) // listed == lax.rem(iota((lanes, spread), 1), sets)
    target = jnp.dot(
        jnp.where(own, picked, 0.0).astype(bf16), gather[...], preferred_element_type=f32
    )
    filtered = [
        jnp.dot(
            mix[which * rows : (which + 1) * rows, :], data, preferred_element_type=f32
        ).astype(bf16)
        for which in range(sets)
    ]

    def beam_unit(unit):
        which, j = divmod(unit, chunks)
        r = which % ranges
        beam = jnp.dot(
            op_t[2 * j * LANES : (2 * j + 2) * LANES, r * rows : (r + 1) * rows],
            filtered[which],
            preferred_element_type=f32,
        )
        re, im = beam[:LANES], beam[LANES:]
        beams[which, j * LANES : (j + 1) * LANES, :] = (re * re + im * im).astype(bf16)

    units = list(range(sets * chunks))
    turns = ITERS * chunks
    done = 0
    for turn in range(ITERS):
        if turn == 0:
            misfit = (target * STEP_SIZE).astype(bf16)
        else:
            predicted = jnp.dot(rounded[...], op_t[...], preferred_element_type=f32)
            misfit = ((target - predicted) * lane_mask[...]).astype(bf16)
        for j in range(chunks):
            left = slice(2 * j * LANES, (2 * j + 1) * LANES)
            right = slice((2 * j + 1) * LANES, (2 * j + 2) * LANES)
            both = slice(2 * j * LANES, (2 * j + 2) * LANES)
            step = jnp.dot(misfit, op[:, both], preferred_element_type=f32)
            z_re, z_im = step[:, :LANES], step[:, LANES:]
            if turn > 0:
                z_re = z_re + estimate[:, left]
                z_im = z_im + estimate[:, right]
            magnitude = z_re * z_re + z_im * z_im
            factor = jnp.maximum(
                1.0 - SHRINK * lax.rsqrt(jnp.maximum(magnitude, SHRINK * SHRINK)), 0.0
            )
            x_re, x_im = z_re * factor, z_im * factor
            if turn < ITERS - 1:
                estimate[:, left] = x_re
                estimate[:, right] = x_im
                rounded[:, left] = x_re.astype(bf16)
                rounded[:, right] = x_im.astype(bf16)
            else:
                rounded[:, j * LANES : (j + 1) * LANES] = (x_re * x_re + x_im * x_im).astype(bf16)
            due = (turn * chunks + j + 1) * len(units) // turns
            while done < due:
                beam_unit(units[done])
                done += 1

    writes = []
    lane_power = [rounded[:, j * LANES : (j + 1) * LANES].T for j in range(chunks)]
    for which in range(sets):
        mine = iota((lanes, pixels), 0) // listed == which
        spots = jnp.where(mine, chosen[...].astype(f32), 0.0).astype(bf16)
        taken = covered[which : which + 1, :] > 0.5
        for j in range(chunks):
            cut = slice(j * LANES, (j + 1) * LANES)
            placed = jnp.dot(lane_power[j], spots, preferred_element_type=f32)
            result[which, cut, :] = jnp.where(
                taken, placed, beams[which, cut, :].astype(f32)
            ).astype(bf16)
        copy = pltpu.make_async_copy(
            result.at[which], power.at[which // ranges, which % ranges], out_sem.at[which]
        )
        copy.start()
        writes.append(copy)
    for copy in writes:
        copy.wait()


def slab(n_az, n_acq, image_stack, steering, wiener_filter, range_group, lay_list, lay_count):
    n = n_az * n_acq
    halves, share, azb_all, ranges, pixels = image_stack.shape
    blocks = azb_all // n
    acqs, elevation = steering.shape[2:]
    rows = halves * acqs
    wide = ranges * rows
    sets = blocks * ranges
    lanes = sets * lay_list.shape[2]
    spread = rows * sets
    bf16 = jnp.bfloat16
    f32 = jnp.float32
    vmem = pl.BlockSpec(memory_space=pltpu.VMEM)
    anywhere = pl.BlockSpec(memory_space=pl.ANY)
    ready = pl.pallas_call(
        functools.partial(exchange_kernel, n_az, n_acq),
        out_shape=[
            pltpu.VMEM((halves, acqs, blocks, ranges, pixels), bf16),
            pltpu.VMEM((wide, 2 * elevation), bf16),
            pltpu.VMEM((2 * elevation, wide), bf16),
            pltpu.VMEM((spread, spread), bf16),
            pltpu.VMEM((lanes, pixels), bf16),
            pltpu.VMEM((lanes, wide), f32),
            pltpu.VMEM((sets, pixels), f32),
            pltpu.VMEM((spread, wide), bf16),
        ],
        in_specs=[anywhere] * 6,
        out_specs=[vmem] * 8,
        scratch_shapes=[
            pltpu.SMEM(range_group.shape, jnp.int32),
            pltpu.SMEM(lay_count.shape, jnp.int32),
            pltpu.VMEM(steering.shape, bf16),
            pltpu.VMEM(wiener_filter.shape, bf16),
            pltpu.VMEM(lay_list.shape, jnp.int32),
            pltpu.SemaphoreType.DMA((n,)),
            pltpu.SemaphoreType.DMA((n,)),
            pltpu.SemaphoreType.DMA((6,)),
        ],
        compiler_params=pltpu.CompilerParams(
            collective_id=0, has_side_effects=True
        ),
        name="exchange",
    )(range_group, lay_count, image_stack, steering, wiener_filter, lay_list)
    return pl.pallas_call(
        functools.partial(solve_kernel, ranges),
        out_shape=jax.ShapeDtypeStruct((blocks, ranges, elevation, pixels), bf16),
        in_specs=[vmem] * 8,
        out_specs=anywhere,
        scratch_shapes=[
            pltpu.VMEM((lanes, 2 * elevation), f32),
            pltpu.VMEM((lanes, 2 * elevation), bf16),
            pltpu.VMEM((sets, elevation, pixels), bf16),
            pltpu.VMEM((sets, elevation, pixels), bf16),
            pltpu.SemaphoreType.DMA((sets,)),
        ],
        compiler_params=pltpu.CompilerParams(vmem_limit_bytes=VMEM_LIMIT),
        name="solve",
    )(*[pltpu.with_memory_space_constraint(array, pltpu.VMEM) for array in ready])


def solution(mesh):
    return jax.shard_map(
        functools.partial(slab, mesh.shape["az"], mesh.shape["acq"]),
        mesh=mesh,
        in_specs=(
            P(None, ("az", "acq"), "groups", "rg", None),
            P("rg", None, None, None),
            P("rg", None, None, None),
            P("rg"),
            P(("groups", "az", "acq"), "rg", None),
            P(("groups", "az", "acq"), "rg"),
        ),
        out_specs=P(("groups", "az", "acq"), "rg", None, None),
        check_vma=False,
    )
```

profile of v0, /device:TPU:1, one launch (start us, length us, event | category | flops | bytes accessed | tf_op | source)
XLA Modules:
  0.0 16.1 jit_solution(10718443020549701925)
XLA Ops:
  0.0 11.1 %exchange.1 = (bf16[2,64,2,2,256]{4,3,2,1,0:T(2,128)(2,1)S(1)}, bf16[256,1024]{1,0:T(8,128)(2,1)S(1)}, bf16[1024,256]{1,0:T(8,128)(2,1)S(1)}, bf16[512,512]{1,0:...) custom-call(s32[2]{0:T(128)} %range_group_in.1, ...), custom_call_target="tpu_custom_call" | custom-call | tf_op jit(solution)/shard_map/exchange/pallas_call | solution.py:284
  11.1 5.0 %solve.1 = bf16[2,2,512,256]{3,2,1,0:T(8,128)(2,1)} custom-call(bf16[2,64,2,2,256]{4,3,2,1,0:T(2,128)(2,1)S(1)} %get-tuple-element.13.recv, bf16[256,1024]{1,0:T(8,128)(2,1)S(1)} %get-tuple-element.14.op, bf16[1024,256]{1,0:T(8,128)(2,1)S(1)} %get-tuple-element.15.op_t, bf16[512,512]{1,0:T(8,128)(2,1)S(1)} %get-tuple-element.16.mix, ...), custom_call_target="tpu_custom_call" | custom-call | tf_op jit(solution)/shard_map/solve/pallas_call | solution.py:313
where the time goes:
time: 16.3 us; the launch traced here: 16.1 us
  Pallas kernels  16.1 us (99%)
    pallas_call x1, Pallas kernels, slab(): pl.pallas_call(functools.partial(exchange_kernel, n_az, n_acq), out_shape...  11.1 us
    pallas_call x1, Pallas kernels, slab(): pl.pallas_call(functools.partial(solve_kernel, ranges), out_shape=jax.Sha...  4.98 us

commit v1 on v0

--- a/solution.py
+++ b/solution.py
@@ -88,6 +88,21 @@
     )
     local.start()
 
+    pl.semaphore_wait(barrier, n - 1)
+    copies = []
+    for offset in range(1, n):
+        there = lax.rem(me + offset, n)
+        copy = pltpu.make_async_remote_copy(
+            src_ref=image.at[:, :, pl.ds(blocks * there, blocks)],
+            dst_ref=recv.at[:, pl.ds(share * me, share)],
+            send_sem=send_sem.at[offset],
+            recv_sem=recv_sem.at[offset],
+            device_id=peer(there),
+            device_id_type=MESH,
+        )
+        copy.start()
+        copies.append(copy)
+
     first_group = lax.axis_index("rg") * groups
     copy_rows = (iota((rows, spread), 1) // sets == iota((rows, spread), 0)).astype(bf16)
     at_row, at_column = iota((spread, wide), 0), iota((spread, wide), 1)
@@ -139,20 +154,6 @@
             chosen[at * listed : (at + 1) * listed, :] = hot.astype(bf16)
             covered[at : at + 1, :] = jnp.sum(hot, axis=0, keepdims=True)
 
-    pl.semaphore_wait(barrier, n - 1)
-    copies = []
-    for offset in range(1, n):
-        there = lax.rem(me + offset, n)
-        copy = pltpu.make_async_remote_copy(
-            src_ref=image.at[:, :, pl.ds(blocks * there, blocks)],
-            dst_ref=recv.at[:, pl.ds(share * me, share)],
-            send_sem=send_sem.at[offset],
-            recv_sem=recv_sem.at[offset],
-            device_id=peer(there),
-            device_id_type=MESH,
-        )
-        copy.start()
-        copies.append(copy)
     local.wait()
     for copy in copies:
         copy.wait()

time: 16.3 us -> 15.6 us (0.957)
  Pallas kernels: 16.1 us -> 15.5 us
    pallas_call x1, Pallas kernels: 11.1 us -> 10.5 us  [slab(): pl.pallas_call(functools.partial(exchange_kernel, n_az, n_acq), out_shape...]
where the time goes in v1:
time: 15.6 us; the launch traced here: 15.5 us
  Pallas kernels  15.5 us (99%)
    pallas_call x1, Pallas kernels, slab(): pl.pallas_call(functools.partial(exchange_kernel, n_az, n_acq), out_shape...  10.5 us
    pallas_call x1, Pallas kernels, slab(): pl.pallas_call(functools.partial(solve_kernel, ranges), out_shape=jax.Sha...  4.98 us

profile of v1, /device:TPU:1, one launch (start us, length us, event | category | flops | bytes accessed | tf_op | source)
XLA Modules:
  0.0 15.5 jit_solution(14741247708987802744)
XLA Ops:
  0.0 10.5 %exchange.1 = (bf16[2,64,2,2,256]{4,3,2,1,0:T(2,128)(2,1)S(1)}, bf16[256,1024]{1,0:T(8,128)(2,1)S(1)}, bf16[1024,256]{1,0:T(8,128)(2,1)S(1)}, bf16[512,512]{1,0:...) custom-call(s32[2]{0:T(128)} %range_group_in.1, ...), custom_call_target="tpu_custom_call" | custom-call | tf_op jit(solution)/shard_map/exchange/pallas_call | solution.py:285
  10.5 5.0 %solve.1 = bf16[2,2,512,256]{3,2,1,0:T(8,128)(2,1)} custom-call(bf16[2,64,2,2,256]{4,3,2,1,0:T(2,128)(2,1)S(1)} %get-tuple-element.13.recv, bf16[256,1024]{1,0:T(8,128)(2,1)S(1)} %get-tuple-element.14.op, bf16[1024,256]{1,0:T(8,128)(2,1)S(1)} %get-tuple-element.15.op_t, bf16[512,512]{1,0:T(8,128)(2,1)S(1)} %get-tuple-element.16.mix, ...), custom_call_target="tpu_custom_call" | custom-call | tf_op jit(solution)/shard_map/solve/pallas_call | solution.py:314

commit v2 on v1

v2 whole, which is shorter than its diff:
```python
import functools

import jax
import jax.numpy as jnp
from jax import lax
from jax.experimental import pallas as pl
from jax.experimental.pallas import tpu as pltpu
from jax.sharding import PartitionSpec as P

ITERS = 8
STEP_SIZE = 0.5
SHRINK = 0.25
LANES = 128
VMEM_LIMIT = 16 * 1024 * 1024
MESH = pl.DeviceIdType.MESH


def iota(shape, axis):
    return lax.broadcasted_iota(jnp.int32, shape, axis)


def exchange_kernel(
    n_az,
    n_acq,
    range_group_in,
    lay_count_in,
    image,
    steering_in,
    wiener_filter_in,
    lay_list_in,
    recv,
    op,
    op_t,
    gram,
    mix,
    chosen,
    covered,
    gather,
    range_group,
    lay_count,
    steering,
    wiener_filter,
    lay_list,
    send_sem,
    recv_sem,
    ready,
    local_sem,
):
    n = n_az * n_acq
    me = lax.axis_index("az") * n_acq + lax.axis_index("acq")
    halves, share, azb_all, ranges, pixels = image.shape
    blocks = azb_all // n
    groups, _, acqs, elevation = steering.shape
    rows = halves * acqs
    listed = lay_list.shape[2]
    sets = blocks * ranges
    spread = rows * sets
    chunks = elevation // LANES
    bf16 = jnp.bfloat16
    f32 = jnp.float32

    def peer(index):
        return {"az": index // n_acq, "acq": index % n_acq}

    barrier = pltpu.get_barrier_semaphore()
    for other in range(1, n):

        @pl.when(other > me)
        def _():
            pl.semaphore_signal(barrier, inc=1, device_id=peer(other), device_id_type=MESH)

    inputs = []
    for at, (source, target) in enumerate(
        (
            (range_group_in, range_group),
            (lay_count_in, lay_count),
            (steering_in, steering),
            (wiener_filter_in, wiener_filter),
            (lay_list_in, lay_list),
        )
    ):
        copy = pltpu.make_async_copy(source, target, local_sem.at[at + 1])
        copy.start()
        inputs.append(copy)
    local = pltpu.make_async_copy(
        image.at[:, :, pl.ds(blocks * me, blocks)],
        recv.at[:, pl.ds(share * me, share)],
        local_sem.at[0],
    )
    local.start()

    def outgoing(b, there):
        return pltpu.make_async_remote_copy(
            src_ref=image.at[:, :, pl.ds(blocks * there, blocks)],
            dst_ref=recv.at[:, pl.ds(share * me, share)],
            send_sem=send_sem.at[b, there],
            recv_sem=recv_sem.at[b, me],
            device_id=peer(there),
            device_id_type=MESH,
        )

    def incoming(b, source):
        return pltpu.make_async_remote_copy(
            src_ref=image.at[:, :, pl.ds(blocks * me, blocks)],
            dst_ref=recv.at[:, pl.ds(share * source, share)],
            send_sem=send_sem.at[b, source],
            recv_sem=recv_sem.at[b, source],
            device_id=peer(source),
            device_id_type=MESH,
        )

    @pl.when(me > 0)
    def _():
        pl.semaphore_wait(barrier, me)

    for other in range(n - 1):

        @pl.when(other < me)
        def _():
            pl.semaphore_signal(ready.at[me], inc=1, device_id=peer(other), device_id_type=MESH)

    for b in range(1):
        for other in range(n - 1):

            @pl.when(other < me)
            def _():
                outgoing(b, other).start()

    for b in range(1):
        for other in range(1, n):

            @pl.when(other > me)
            def _():
                if b == 0:
                    pl.semaphore_wait(ready.at[other], 1)
                outgoing(b, other).start()

    copy_rows = (iota((rows, spread), 1) // sets == iota((rows, spread), 0)).astype(bf16)
    gather[...] = (iota((spread, rows), 0) // sets == iota((spread, rows), 1)).astype(bf16)
    for copy in inputs:
        copy.wait()
    first_group = lax.axis_index("rg") * groups
    for r in range(ranges):
        group = range_group[r] - first_group
        steer = steering[0]
        filt = wiener_filter[0]
        for g in range(1, groups):
            steer = jnp.where(group == g, steering[g], steer)
            filt = jnp.where(group == g, wiener_filter[g], filt)
        re, im = steer[0], steer[1]
        for j in range(chunks):
            cut = slice(j * LANES, (j + 1) * LANES)
            left = slice(2 * j * LANES, (2 * j + 1) * LANES)
            right = slice((2 * j + 1) * LANES, (2 * j + 2) * LANES)
            op[r, :acqs, left] = re[:, cut]
            op[r, :acqs, right] = -im[:, cut]
            op[r, acqs:, left] = im[:, cut]
            op[r, acqs:, right] = re[:, cut]
        upper = jnp.concatenate([filt[0], -filt[1]], axis=1)
        lower = jnp.concatenate([filt[1], filt[0]], axis=1)
        filter_matrix = jnp.concatenate([upper, lower], axis=0)
        repeated = jnp.dot(filter_matrix, copy_rows, preferred_element_type=f32)
        for b in range(blocks):
            keep = lax.rem(iota((rows, spread), 1), sets) == b * ranges + r
            at = (b * ranges + r) * rows
            mix[at : at + rows, :] = jnp.where(keep, repeated, 0.0).astype(bf16)
        for j in range(2 * chunks):
            op_t[r, j * LANES : (j + 1) * LANES, :] = op[r, :, j * LANES : (j + 1) * LANES].T
        for j in range(chunks):
            left = op_t[r, 2 * j * LANES : (2 * j + 1) * LANES, :]
            part = jnp.dot(left, op[r], preferred_element_type=f32)
            gram[r, j * LANES : (j + 1) * LANES, :] = (-STEP_SIZE * part).astype(bf16)

    diagonal = iota((listed, listed), 0) == iota((listed, listed), 1)
    for b in range(blocks):
        for r in range(ranges):
            entries = lay_list[b, r : r + 1, :].astype(f32)
            column = jnp.sum(jnp.where(diagonal, entries, 0.0), axis=1, keepdims=True)
            alive = iota((listed, pixels), 0) < lay_count[b, r]
            hit = (iota((listed, pixels), 1).astype(f32) == column) & alive
            hot = jnp.where(hit, 1.0, 0.0)
            at = r * blocks + b
            chosen[at * listed : (at + 1) * listed, :] = hot.astype(bf16)
            at = b * ranges + r
            covered[at : at + 1, :] = jnp.sum(hot, axis=0, keepdims=True)

    local.wait()
    for b in range(1):
        for other in range(n):

            @pl.when(other != me)
            def _():
                incoming(b, other).wait_recv()
                outgoing(b, other).wait_send()


def solve_kernel(
    blocks,
    recv,
    op,
    op_t,
    gram,
    mix,
    chosen,
    covered,
    gather,
    power,
    start,
    estimate,
    rounded,
    beams,
    result,
    out_sem,
):
    ranges, rows, wide = op.shape
    spread = mix.shape[0]
    sets = spread // rows
    chunks = wide // (2 * LANES)
    lanes, pixels = chosen.shape
    listed = lanes // sets
    group = lanes // ranges
    bf16 = jnp.bfloat16
    f32 = jnp.float32

    data = recv[...].reshape(spread, pixels)
    picked = lax.dot_general(
        chosen[...], data, (((1,), (1,)), ((), ())), preferred_element_type=f32
    )
    lane, column = iota((lanes, spread), 0), lax.rem(iota((lanes, spread), 1), sets)
    lane_set = lax.rem(lane // listed, blocks) * ranges + lane // group
    target = jnp.dot(
        jnp.where(lane_set == column, picked, 0.0).astype(bf16),
        gather[...],
        preferred_element_type=f32,
    )
    target = (target * (STEP_SIZE / SHRINK)).astype(bf16)
    filtered = [
        jnp.dot(
            mix[which * rows : (which + 1) * rows, :], data, preferred_element_type=f32
        ).astype(bf16)
        for which in range(sets)
    ]

    def beam_unit(unit):
        which, j = divmod(unit, chunks)
        beam = jnp.dot(
            op_t[which % ranges, 2 * j * LANES : (2 * j + 2) * LANES, :],
            filtered[which],
            preferred_element_type=f32,
        )
        re, im = beam[:LANES], beam[LANES:]
        beams[which, j * LANES : (j + 1) * LANES, :] = (re * re + im * im).astype(bf16)

    units = list(range(sets * chunks))
    turns = ITERS * chunks * ranges
    turned = 0
    done = 0
    for turn in range(ITERS):
        for r in range(ranges):
            old = rounded[(turn + 1) % 2, r] if turn > 0 else None
            for j in range(chunks):
                left = slice(2 * j * LANES, (2 * j + 1) * LANES)
                right = slice((2 * j + 1) * LANES, (2 * j + 2) * LANES)
                both = slice(2 * j * LANES, (2 * j + 2) * LANES)
                cut = slice(j * LANES, (j + 1) * LANES)
                if turn == 0:
                    step = jnp.dot(
                        target[r * group : (r + 1) * group],
                        op[r, :, both],
                        preferred_element_type=f32,
                    )
                    z_re, z_im = step[:, :LANES], step[:, LANES:]
                    start[r, :, left] = z_re
                    start[r, :, right] = z_im
                else:
                    step = jnp.dot(old, gram[r, :, both], preferred_element_type=f32)
                    z_re = estimate[r, :, left] + (step[:group, :LANES] - step[group:, LANES:])
                    z_im = estimate[r, :, right] + (step[:group, LANES:] + step[group:, :LANES])
                magnitude = z_re * z_re + z_im * z_im
                factor = jnp.maximum(1.0 - lax.rsqrt(jnp.maximum(magnitude, 1.0)), 0.0)
                x_re, x_im = z_re * factor, z_im * factor
                if turn < ITERS - 1:
                    estimate[r, :, left] = x_re + start[r, :, left]
                    estimate[r, :, right] = x_im + start[r, :, right]
                    rounded[turn % 2, r, :group, cut] = x_re.astype(bf16)
                    rounded[turn % 2, r, group:, cut] = x_im.astype(bf16)
                else:
                    level = (x_re * x_re + x_im * x_im) * (SHRINK * SHRINK)
                    rounded[turn % 2, r, :group, cut] = level.astype(bf16)
                turned += 1
                due = turned * len(units) // turns
                while done < due:
                    beam_unit(units[done])
                    done += 1

    last = (ITERS - 1) % 2
    writes = []
    for r in range(ranges):
        lane_power = [
            rounded[last, r, :group, j * LANES : (j + 1) * LANES].T for j in range(chunks)
        ]
        for b in range(blocks):
            which = b * ranges + r
            mine = iota((group, pixels), 0) // listed == b
            spots = chosen[r * group : (r + 1) * group, :].astype(f32)
            spots = jnp.where(mine, spots, 0.0).astype(bf16)
            taken = covered[which : which + 1, :] > 0.5
            for j in range(chunks):
                cut = slice(j * LANES, (j + 1) * LANES)
                placed = jnp.dot(lane_power[j], spots, preferred_element_type=f32)
                result[which, cut, :] = jnp.where(
                    taken, placed, beams[which, cut, :].astype(f32)
                ).astype(bf16)
            copy = pltpu.make_async_copy(result.at[which], power.at[b, r], out_sem.at[which])
            copy.start()
            writes.append(copy)
    for copy in writes:
        copy.wait()


def slab(n_az, n_acq, image_stack, steering, wiener_filter, range_group, lay_list, lay_count):
    n = n_az * n_acq
    halves, share, azb_all, ranges, pixels = image_stack.shape
    blocks = azb_all // n
    acqs, elevation = steering.shape[2:]
    rows = halves * acqs
    wide = 2 * elevation
    sets = blocks * ranges
    lanes = sets * lay_list.shape[2]
    spread = rows * sets
    bf16 = jnp.bfloat16
    f32 = jnp.float32
    vmem = pl.BlockSpec(memory_space=pltpu.VMEM)
    anywhere = pl.BlockSpec(memory_space=pl.ANY)
    ready = pl.pallas_call(
        functools.partial(exchange_kernel, n_az, n_acq),
        out_shape=[
            pltpu.VMEM((halves, acqs, blocks, ranges, pixels), bf16),
            pltpu.VMEM((ranges, rows, wide), bf16),
            pltpu.VMEM((ranges, wide, rows), bf16),
            pltpu.VMEM((ranges, elevation, wide), bf16),
            pltpu.VMEM((spread, spread), bf16),
            pltpu.VMEM((lanes, pixels), bf16),
            pltpu.VMEM((sets, pixels), f32),
            pltpu.VMEM((spread, rows), bf16),
        ],
        in_specs=[pl.BlockSpec(memory_space=pltpu.HBM)] * 6,
        out_specs=[vmem] * 8,
        scratch_shapes=[
            pltpu.SMEM(range_group.shape, jnp.int32),
            pltpu.SMEM(lay_count.shape, jnp.int32),
            pltpu.VMEM(steering.shape, bf16),
            pltpu.VMEM(wiener_filter.shape, bf16),
            pltpu.VMEM(lay_list.shape, jnp.int32),
            pltpu.SemaphoreType.DMA((blocks, n)),
            pltpu.SemaphoreType.DMA((blocks, n)),
            pltpu.SemaphoreType.REGULAR((n,)),
            pltpu.SemaphoreType.DMA((6,)),
        ],
        compiler_params=pltpu.CompilerParams(
            collective_id=0, has_side_effects=True, vmem_limit_bytes=VMEM_LIMIT
        ),
        name="exchange",
    )(range_group, lay_count, image_stack, steering, wiener_filter, lay_list)
    return pl.pallas_call(
        functools.partial(solve_kernel, blocks),
        out_shape=jax.ShapeDtypeStruct((blocks, ranges, elevation, pixels), bf16),
        in_specs=[vmem] * 8,
        out_specs=anywhere,
        scratch_shapes=[
            pltpu.VMEM((ranges, lanes // ranges, wide), f32),
            pltpu.VMEM((ranges, lanes // ranges, wide), f32),
            pltpu.VMEM((2, ranges, 2 * (lanes // ranges), elevation), bf16),
            pltpu.VMEM((sets, elevation, pixels), bf16),
            pltpu.VMEM((sets, elevation, pixels), bf16),
            pltpu.SemaphoreType.DMA((sets,)),
        ],
        compiler_params=pltpu.CompilerParams(vmem_limit_bytes=VMEM_LIMIT),
        name="solve",
    )(*[pltpu.with_memory_space_constraint(array, pltpu.VMEM) for array in ready])


def solution(mesh):
    return jax.shard_map(
        functools.partial(slab, mesh.shape["az"], mesh.shape["acq"]),
        mesh=mesh,
        in_specs=(
            P(None, ("az", "acq"), "groups", "rg", None),
            P("rg", None, None, None),
            P("rg", None, None, None),
            P("rg"),
            P(("groups", "az", "acq"), "rg", None),
            P(("groups", "az", "acq"), "rg"),
        ),
        out_specs=P(("groups", "az", "acq"), "rg", None, None),
        check_vma=False,
    )
```

time: 15.6 us -> 19.5 us (1.25)
  local copies, waits for them, and re-layouts: 0 us -> 4.75 us
  Pallas kernels: 15.5 us -> 14.5 us
    unnamed x0 -> x12, local copies, waits for them, and re-layouts: none -> 4.75 us
    pallas_call x1, Pallas kernels: 4.98 us -> 4.45 us  [slab(): pl.pallas_call(functools.partial(solve_kernel, blocks), out_shape=jax.Sha...]
    pallas_call x1, Pallas kernels: 10.5 us -> 10 us  [slab(): pl.pallas_call(functools.partial(exchange_kernel, n_az, n_acq), out_shape...]
where the time goes in v2:
time: 19.5 us; the launch traced here: 19.2 us
  Pallas kernels  14.5 us (74%)
  local copies, waits for them, and re-layouts  4.75 us (24%)
    pallas_call x1, Pallas kernels, slab(): pl.pallas_call(functools.partial(exchange_kernel, n_az, n_acq), out_shape...  10 us
    unnamed x12, local copies, waits for them, and re-layouts  4.75 us
    pallas_call x1, Pallas kernels, slab(): pl.pallas_call(functools.partial(solve_kernel, blocks), out_shape=jax.Sha...  4.45 us

profile of v2, /device:TPU:1, one launch (start us, length us, event | category | flops | bytes accessed | tf_op | source)
XLA Modules:
  0.0 19.2 jit_solution(599145693310267325)
XLA Ops:
  0.0 0.0 copy-start
  0.0 0.9 %copy-done = bf16[2,8,16,2,256]{4,3,2,1,0:T(2,128)(2,1)S(1)} copy-done((bf16[2,8,16,2,256]{4,3,2,1,0:T(2,128)(2,1)S(1)}, bf16[2,8,16,2,256]{4,3,2,1,0:T(2,128)(2,1)}, u32[]{:S(2)}) %copy-start) | copy-done | bytes 262168
  1.0 0.0 copy-start.1
  1.0 0.9 %copy-done.1 = bf16[2,2,64,512]{3,2,1,0:T(8,128)(2,1)S(1)} copy-done((bf16[2,2,64,512]{3,2,1,0:T(8,128)(2,1)S(1)}, bf16[2,2,64,512]{3,2,1,0:T(8,128)(2,1)}, u32[]{:S(2)}) %copy-start.1) | copy-done | bytes 262168
  1.9 0.0 copy-start.2
  1.9 0.8 %copy-done.2 = bf16[2,2,64,64]{3,2,1,0:T(8,128)(2,1)S(1)} copy-done((bf16[2,2,64,64]{3,2,1,0:T(8,128)(2,1)S(1)}, bf16[2,2,64,64]{3,2,1,0:T(8,128)(2,1)}, u32[]{:S(2)}) %copy-start.2) | copy-done | bytes 32792
  2.7 0.0 copy-start.3
  2.7 0.7 %copy-done.3 = s32[2,2,32]{2,1,0:T(2,128)S(1)} copy-done((s32[2,2,32]{2,1,0:T(2,128)S(1)}, s32[2,2,32]{2,1,0:T(2,128)}, u32[]{:S(2)}) %copy-start.3) | copy-done | bytes 536
  3.4 0.0 copy-start.4
  3.4 0.7 %copy-done.4 = s32[2,2]{1,0:T(2,128)S(1)} copy-done((s32[2,2]{1,0:T(2,128)S(1)}, s32[2,2]{1,0:T(2,128)}, u32[]{:S(2)}) %copy-start.4) | copy-done | bytes 40
  4.1 0.0 copy-start.5
  4.1 0.7 %copy-done.5 = s32[2]{0:T(128)S(1)} copy-done((s32[2]{0:T(128)S(1)}, s32[2]{0:T(128)}, u32[]{:S(2)}) %copy-start.5) | copy-done | bytes 32
  4.8 10.0 %exchange.1 = (bf16[2,64,2,2,256]{4,3,2,1,0:T(2,128)(2,1)S(1)}, bf16[2,128,1024]{2,1,0:T(8,128)(2,1)S(1)}, bf16[2,1024,128]{2,1,0:T(8,128)(2,1)S(1)}, bf16[2,512...) custom-call(s32[2]{0:T(128)S(1)} %copy-done.5, ...), custom_call_target="tpu_custom_call" | custom-call | tf_op jit(solution)/shard_map/exchange/pallas_call | solution.py:335
  14.8 4.5 %solve.1 = bf16[2,2,512,256]{3,2,1,0:T(8,128)(2,1)} custom-call(bf16[2,64,2,2,256]{4,3,2,1,0:T(2,128)(2,1)S(1)} %get-tuple-element.13.recv, bf16[2,128,1024]{2,1,0:T(8,128)(2,1)S(1)} %get-tuple-element.14.op, bf16[2,1024,128]{2,1,0:T(8,128)(2,1)S(1)} %get-tuple-element.15.op_t, bf16[2,512,1024]{2,1,0:T(8,128)(2,1)S(1)} %get-tuple-element.16.gram, ...), custom_call_target="tpu_custom_call" | custom-call | tf_op jit(solution)/shard_map/solve/pallas_call | solution.py:365
Async XLA Ops:
  0.0 0.9 %copy-start = (bf16[2,8,16,2,256]{4,3,2,1,0:T(2,128)(2,1)S(1)}, bf16[2,8,16,2,256]{4,3,2,1,0:T(2,128)(2,1)}, u32[]{:S(2)}) copy-start(bf16[2,8,16,2,256]{4,3,2,1,0:T(2,128)(2,1)} %image.1) | copy-start | bytes 786436
  1.0 0.9 %copy-start.1 = (bf16[2,2,64,512]{3,2,1,0:T(8,128)(2,1)S(1)}, bf16[2,2,64,512]{3,2,1,0:T(8,128)(2,1)}, u32[]{:S(2)}) copy-start(bf16[2,2,64,512]{3,2,1,0:T(8,128)(2,1)} %steering_in.1) | copy-start | bytes 786436
  1.9 0.8 %copy-start.2 = (bf16[2,2,64,64]{3,2,1,0:T(8,128)(2,1)S(1)}, bf16[2,2,64,64]{3,2,1,0:T(8,128)(2,1)}, u32[]{:S(2)}) copy-start(bf16[2,2,64,64]{3,2,1,0:T(8,128)(2,1)} %wiener_filter_in.1) | copy-start | bytes 98308
  2.7 0.7 %copy-start.3 = (s32[2,2,32]{2,1,0:T(2,128)S(1)}, s32[2,2,32]{2,1,0:T(2,128)}, u32[]{:S(2)}) copy-start(s32[2,2,32]{2,1,0:T(2,128)} %lay_list_in.1) | copy-start | bytes 1540
  3.4 0.7 %copy-start.4 = (s32[2,2]{1,0:T(2,128)S(1)}, s32[2,2]{1,0:T(2,128)}, u32[]{:S(2)}) copy-start(s32[2,2]{1,0:T(2,128)} %lay_count_in.1) | copy-start | bytes 52
  4.1 0.7 %copy-start.5 = (s32[2]{0:T(128)S(1)}, s32[2]{0:T(128)}, u32[]{:S(2)}) copy-start(s32[2]{0:T(128)} %range_group_in.1) | copy-start | bytes 28

commit v3 on v2

--- a/solution.py
+++ b/solution.py
@@ -361,7 +361,7 @@
             collective_id=0, has_side_effects=True, vmem_limit_bytes=VMEM_LIMIT
         ),
         name="exchange",
-    )(range_group, lay_count, image_stack, steering, wiener_filter, lay_list)
+    )(*[pltpu.with_memory_space_constraint(array, pltpu.HBM) for array in (range_group, lay_count, image_stack, steering, wiener_filter, lay_list)])
     return pl.pallas_call(
         functools.partial(solve_kernel, blocks),
         out_shape=jax.ShapeDtypeStruct((blocks, ranges, elevation, pixels), bf16),

time: 19.5 us -> 14.8 us (0.76)
  local copies, waits for them, and re-layouts: 4.75 us -> 0 us
    unnamed x12 -> x0, local copies, waits for them, and re-layouts: 4.75 us -> none
    pallas_call x1, Pallas kernels: 10 us -> 10.2 us  [slab(): pl.pallas_call(functools.partial(exchange_kernel, n_az, n_acq), out_shape...]
where the time goes in v3:
time: 14.8 us; the launch traced here: 14.6 us
  Pallas kernels  14.6 us (99%)
    pallas_call x1, Pallas kernels, slab(): pl.pallas_call(functools.partial(exchange_kernel, n_az, n_acq), out_shape...  10.2 us
    pallas_call x1, Pallas kernels, slab(): pl.pallas_call(functools.partial(solve_kernel, blocks), out_shape=jax.Sha...  4.41 us

profile of v3, /device:TPU:1, one launch (start us, length us, event | category | flops | bytes accessed | tf_op | source)
XLA Modules:
  0.0 14.6 jit_solution(17713376715968766053)
XLA Ops:
  0.0 10.2 %exchange.1 = (bf16[2,64,2,2,256]{4,3,2,1,0:T(2,128)(2,1)S(1)}, bf16[2,128,1024]{2,1,0:T(8,128)(2,1)S(1)}, bf16[2,1024,128]{2,1,0:T(8,128)(2,1)S(1)}, bf16[2,512...) custom-call(s32[2]{0:T(128)} %range_group_in.1, ...), custom_call_target="tpu_custom_call" | custom-call | tf_op jit(solution)/shard_map/exchange/pallas_call | solution.py:335
  10.2 4.4 %solve.1 = bf16[2,2,512,256]{3,2,1,0:T(8,128)(2,1)} custom-call(bf16[2,64,2,2,256]{4,3,2,1,0:T(2,128)(2,1)S(1)} %get-tuple-element.13.recv, bf16[2,128,1024]{2,1,0:T(8,128)(2,1)S(1)} %get-tuple-element.14.op, bf16[2,1024,128]{2,1,0:T(8,128)(2,1)S(1)} %get-tuple-element.15.op_t, bf16[2,512,1024]{2,1,0:T(8,128)(2,1)S(1)} %get-tuple-element.16.gram, ...), custom_call_target="tpu_custom_call" | custom-call | tf_op jit(solution)/shard_map/solve/pallas_call | solution.py:365

commit v4 on v3

--- a/solution.py
+++ b/solution.py
@@ -41,9 +41,11 @@
     steering,
     wiener_filter,
     lay_list,
+    staged,
     send_sem,
     recv_sem,
     ready,
+    gate,
     local_sem,
 ):
     n = n_az * n_acq
@@ -58,6 +60,8 @@
     chunks = elevation // LANES
     bf16 = jnp.bfloat16
     f32 = jnp.float32
+
+    half = n_az // 2 * n_acq
 
     def peer(index):
         return {"az": index // n_acq, "acq": index % n_acq}
@@ -89,9 +93,15 @@
     )
     local.start()
 
-    def outgoing(b, there):
+    stage = pltpu.make_async_copy(image, staged, local_sem.at[6])
+
+    @pl.when(me < half)
+    def _():
+        stage.start()
+
+    def outgoing(b, there, source=image):
         return pltpu.make_async_remote_copy(
-            src_ref=image.at[:, :, pl.ds(blocks * there, blocks)],
+            src_ref=source.at[:, :, pl.ds(blocks * there, blocks)],
             dst_ref=recv.at[:, pl.ds(share * me, share)],
             send_sem=send_sem.at[b, there],
             recv_sem=recv_sem.at[b, me],
@@ -119,21 +129,37 @@
         def _():
             pl.semaphore_signal(ready.at[me], inc=1, device_id=peer(other), device_id_type=MESH)
 
-    for b in range(1):
-        for other in range(n - 1):
-
-            @pl.when(other < me)
-            def _():
-                outgoing(b, other).start()
-
-    for b in range(1):
-        for other in range(1, n):
-
-            @pl.when(other > me)
-            def _():
-                if b == 0:
-                    pl.semaphore_wait(ready.at[other], 1)
-                outgoing(b, other).start()
+    az = me // n_acq
+    middle = n_az // 2
+    inner = (az >= middle) & (az + 1 < n_az)
+    outer = (az > middle) & (az < n_az)
+
+    def held(other):
+        return (inner & (other // n_acq == middle - 1)) | (outer & (other >= n_acq))
+
+    for other in range(n - 1):
+
+        @pl.when((other < me) & jnp.logical_not(held(other)))
+        def _():
+            outgoing(0, other).start()
+
+    @pl.when(me < half)
+    def _():
+        stage.wait()
+
+    for other in range(1, n):
+
+        @pl.when(other > me)
+        def _():
+            pl.semaphore_wait(ready.at[other], 1)
+
+        @pl.when((other > me) & (me < half))
+        def _():
+            outgoing(0, other, staged).start()
+
+        @pl.when((other > me) & (me >= half))
+        def _():
+            outgoing(0, other).start()
 
     copy_rows = (iota((rows, spread), 1) // sets == iota((rows, spread), 0)).astype(bf16)
     gather[...] = (iota((spread, rows), 0) // sets == iota((spread, rows), 1)).astype(bf16)
@@ -184,14 +210,32 @@
             at = b * ranges + r
             covered[at : at + 1, :] = jnp.sum(hot, axis=0, keepdims=True)
 
+    @pl.when(outer)
+    def _():
+        for near in range(n_acq):
+            outgoing(0, near).wait_send()
+        pl.semaphore_signal(gate, inc=1, device_id=peer(me - n_acq), device_id_type=MESH)
+
+    @pl.when(inner)
+    def _():
+        pl.semaphore_wait(gate, 1)
+
+    for other in range(n - 1):
+
+        @pl.when((other < me) & held(other))
+        def _():
+            outgoing(0, other).start()
+
     local.wait()
-    for b in range(1):
-        for other in range(n):
-
-            @pl.when(other != me)
-            def _():
-                incoming(b, other).wait_recv()
-                outgoing(b, other).wait_send()
+    for other in range(n):
+
+        @pl.when(other != me)
+        def _():
+            incoming(0, other).wait_recv()
+
+        @pl.when((other != me) & jnp.logical_not(outer) if other < n_acq else other != me)
+        def _():
+            outgoing(0, other).wait_send()
 
 
 def solve_kernel(
@@ -352,10 +396,12 @@
             pltpu.VMEM(steering.shape, bf16),
             pltpu.VMEM(wiener_filter.shape, bf16),
             pltpu.VMEM(lay_list.shape, jnp.int32),
+            pltpu.VMEM(image_stack.shape, bf16),
             pltpu.SemaphoreType.DMA((blocks, n)),
             pltpu.SemaphoreType.DMA((blocks, n)),
             pltpu.SemaphoreType.REGULAR((n,)),
-            pltpu.SemaphoreType.DMA((6,)),
+            pltpu.SemaphoreType.REGULAR,
+            pltpu.SemaphoreType.DMA((7,)),
         ],
         compiler_params=pltpu.CompilerParams(
             collective_id=0, has_side_effects=True, vmem_limit_bytes=VMEM_LIMIT

time: 14.8 us -> 13.9 us (0.939)
  the two profiles are of different devices: /device:TPU:1 before, /device:TPU:31 now
where the time goes in v4:
time: 13.9 us; the launch traced here: 13.8 us
  Pallas kernels  13.8 us (99%)
    pallas_call x1, Pallas kernels, slab(): pl.pallas_call(functools.partial(exchange_kernel, n_az, n_acq), out_shape...  9.37 us
    pallas_call x1, Pallas kernels, slab(): pl.pallas_call(functools.partial(solve_kernel, blocks), out_shape=jax.Sha...  4.41 us

profile of v4, /device:TPU:31, one launch (start us, length us, event | category | flops | bytes accessed | tf_op | source)
XLA Modules:
  0.0 13.8 jit_solution(16621032157788662533)
XLA Ops:
  0.0 9.4 %exchange.1 = (bf16[2,64,2,2,256]{4,3,2,1,0:T(2,128)(2,1)S(1)}, bf16[2,128,1024]{2,1,0:T(8,128)(2,1)S(1)}, bf16[2,1024,128]{2,1,0:T(8,128)(2,1)S(1)}, bf16[2,512...) custom-call(s32[2]{0:T(128)} %range_group_in.1, ...), custom_call_target="tpu_custom_call" | custom-call | tf_op jit(solution)/shard_map/exchange/pallas_call | solution.py:379
  9.4 4.4 %solve.1 = bf16[2,2,512,256]{3,2,1,0:T(8,128)(2,1)} custom-call(bf16[2,64,2,2,256]{4,3,2,1,0:T(2,128)(2,1)S(1)} %get-tuple-element.13.recv, bf16[2,128,1024]{2,1,0:T(8,128)(2,1)S(1)} %get-tuple-element.14.op, bf16[2,1024,128]{2,1,0:T(8,128)(2,1)S(1)} %get-tuple-element.15.op_t, bf16[2,512,1024]{2,1,0:T(8,128)(2,1)S(1)} %get-tuple-element.16.gram, ...), custom_call_target="tpu_custom_call" | custom-call | tf_op jit(solution)/shard_map/solve/pallas_call | solution.py:411

commit v5 on v4

--- a/solution.py
+++ b/solution.py
@@ -278,12 +278,13 @@
         preferred_element_type=f32,
     )
     target = (target * (STEP_SIZE / SHRINK)).astype(bf16)
-    filtered = [
-        jnp.dot(
+    filtered = []
+    for which in range(sets):
+        product = jnp.dot(
             mix[which * rows : (which + 1) * rows, :], data, preferred_element_type=f32
-        ).astype(bf16)
-        for which in range(sets)
-    ]
+        )
+        taken = covered[which : which + 1, :] > 0.5
+        filtered.append(jnp.where(taken, 0.0, product).astype(bf16))
 
     def beam_unit(unit):
         which, j = divmod(unit, chunks)
@@ -317,7 +318,9 @@
                     start[r, :, left] = z_re
                     start[r, :, right] = z_im
                 else:
-                    step = jnp.dot(old, gram[r, :, both], preferred_element_type=f32)
+                    mid = wide // 4
+                    step = jnp.dot(old[:, :mid], gram[r, :mid, both], preferred_element_type=f32)
+                    step = step + jnp.dot(old[:, mid:], gram[r, mid:, both], preferred_element_type=f32)
                     z_re = estimate[r, :, left] + (step[:group, :LANES] - step[group:, LANES:])
                     z_im = estimate[r, :, right] + (step[:group, LANES:] + step[group:, :LANES])
                 magnitude = z_re * z_re + z_im * z_im
@@ -348,13 +351,10 @@
             mine = iota((group, pixels), 0) // listed == b
             spots = chosen[r * group : (r + 1) * group, :].astype(f32)
             spots = jnp.where(mine, spots, 0.0).astype(bf16)
-            taken = covered[which : which + 1, :] > 0.5
             for j in range(chunks):
                 cut = slice(j * LANES, (j + 1) * LANES)
                 placed = jnp.dot(lane_power[j], spots, preferred_element_type=f32)
-                result[which, cut, :] = jnp.where(
-                    taken, placed, beams[which, cut, :].astype(f32)
-                ).astype(bf16)
+                result[which, cut, :] = (beams[which, cut, :].astype(f32) + placed).astype(bf16)
             copy = pltpu.make_async_copy(result.at[which], power.at[b, r], out_sem.at[which])
             copy.start()
             writes.append(copy)

time: 13.9 us -> 13.9 us (level)
  no operation moved by 1% of the time
where the time goes in v5:
time: 13.9 us; the launch traced here: 13.8 us
  Pallas kernels  13.7 us (99%)
    pallas_call x1, Pallas kernels, slab(): pl.pallas_call(functools.partial(exchange_kernel, n_az, n_acq), out_shape...  9.37 us
    pallas_call x1, Pallas kernels, slab(): pl.pallas_call(functools.partial(solve_kernel, blocks), out_shape=jax.Sha...  4.37 us

profile of v5, /device:TPU:31, one launch (start us, length us, event | category | flops | bytes accessed | tf_op | source)
XLA Modules:
  0.0 13.8 jit_solution(12879233261698254354)
XLA Ops:
  0.0 9.4 %exchange.1 = (bf16[2,64,2,2,256]{4,3,2,1,0:T(2,128)(2,1)S(1)}, bf16[2,128,1024]{2,1,0:T(8,128)(2,1)S(1)}, bf16[2,1024,128]{2,1,0:T(8,128)(2,1)S(1)}, bf16[2,512...) custom-call(s32[2]{0:T(128)} %range_group_in.1, ...), custom_call_target="tpu_custom_call" | custom-call | tf_op jit(solution)/shard_map/exchange/pallas_call | solution.py:379
  9.4 4.4 %solve.1 = bf16[2,2,512,256]{3,2,1,0:T(8,128)(2,1)} custom-call(bf16[2,64,2,2,256]{4,3,2,1,0:T(2,128)(2,1)S(1)} %get-tuple-element.13.recv, bf16[2,128,1024]{2,1,0:T(8,128)(2,1)S(1)} %get-tuple-element.14.op, bf16[2,1024,128]{2,1,0:T(8,128)(2,1)S(1)} %get-tuple-element.15.op_t, bf16[2,512,1024]{2,1,0:T(8,128)(2,1)S(1)} %get-tuple-element.16.gram, ...), custom_call_target="tpu_custom_call" | custom-call | tf_op jit(solution)/shard_map/solve/pallas_call | solution.py:411
